TPU v7x, 64 devices: a 2x2x8 block of a 4x4x8 slice. The times are simulated.
64 devices in a mesh: tasks: 4 (over x, y), group: 16 (over z, core).
Axes of the slice: x: 2, y: 2, z: 8, core: 2. Of those that a mesh axis runs over, the one named last changes fastest.
The devices are a block of a 4x4x8 slice.
Arguments:
- points: bfloat16 [131072, 512], P(('tasks', 'group')), parts along dimension 0
- vectors: bfloat16 [131072, 16], P(('tasks', 'group')), parts along dimension 0
- lengthscale: float32 [1], replicated
- outscale: float32 [1], replicated
Outputs:
- output: float32 [131072, 16], P(('tasks', 'group')), parts along dimension 0
There are 4 independent parts. A program takes and returns all parts, laid end to end along the dimension named above; an argument that names none is the same for every part.
All inputs are finite; a program needn't handle non-finite values.
Results may differ from a plain program's by a relative error of at most 0.001.
Values are sent between devices in bfloat16 or wider.
A program may use at most 768 MiB of HBM per device.

v0:
```python
import jax
import jax.numpy as jnp
from jax import lax
from jax.sharding import PartitionSpec as P


def row_norms(x_rows):
    return jnp.sum(jnp.square(x_rows.astype(jnp.float32)), axis=1)


def kernel_block(x_rows, norm_rows, x_cols, norm_cols, two_ell_sq, out_scale):
    gram_mat = jnp.einsum('nd,md->nm', x_rows, x_cols, preferred_element_type=jnp.float32)
    sq_dist = jnp.maximum(norm_rows[:, None] + norm_cols[None, :] - 2.0 * gram_mat, 0.0)
    return (out_scale * jnp.exp(-sq_dist / two_ell_sq)).astype(jnp.bfloat16)


def solution(mesh):
    n_group = mesh.shape['group']
    half_way = n_group // 2
    shift_left = [(source_idx, (source_idx - 1) % n_group) for source_idx in range(n_group)]
    send_back = [(source_idx, (source_idx + half_way - 1) % n_group) for source_idx in range(n_group)]
    row_spec = P(('tasks', 'group'), None)

    def local_fn(x_loc, v_loc, lengthscale, outscale):
        two_ell_sq = 2.0 * jnp.square(lengthscale[0])
        out_scale = outscale[0]
        norm_loc = row_norms(x_loc)

        def pair_step(x_vis, v_vis, y_acc, partner_acc):
            kern_pair = kernel_block(x_loc, norm_loc, x_vis, row_norms(x_vis), two_ell_sq, out_scale)
            y_acc = y_acc + jnp.dot(kern_pair, v_vis, preferred_element_type=jnp.float32)
            partner_acc = partner_acc + jnp.einsum('nm,nr->mr', kern_pair, v_loc, preferred_element_type=jnp.float32)
            return y_acc, partner_acc

        def loop_body(step_idx, carry):
            x_vis, v_vis, y_acc, partner_acc = carry
            x_vis = lax.ppermute(x_vis, 'group', shift_left)
            v_vis = lax.ppermute(v_vis, 'group', shift_left)
            partner_acc = lax.ppermute(partner_acc, 'group', shift_left)
            y_acc, partner_acc = pair_step(x_vis, v_vis, y_acc, partner_acc)
            return x_vis, v_vis, y_acc, partner_acc

        kern_diag = kernel_block(x_loc, norm_loc, x_loc, norm_loc, two_ell_sq, out_scale)
        y_acc = jnp.dot(kern_diag, v_loc, preferred_element_type=jnp.float32)
        x_vis = lax.ppermute(x_loc, 'group', shift_left)
        v_vis = lax.ppermute(v_loc, 'group', shift_left)
        y_acc, partner_acc = pair_step(x_vis, v_vis, y_acc, jnp.zeros(y_acc.shape, jnp.float32))
        x_vis, v_vis, y_acc, partner_acc = lax.fori_loop(2, half_way, loop_body, (x_vis, v_vis, y_acc, partner_acc))
        y_acc = y_acc + lax.ppermute(partner_acc, 'group', send_back)
        x_vis = lax.ppermute(x_vis, 'group', shift_left)
        v_vis = lax.ppermute(v_vis, 'group', shift_left)
        kern_far = kernel_block(x_loc, norm_loc, x_vis, row_norms(x_vis), two_ell_sq, out_scale)
        return y_acc + jnp.dot(kern_far, v_vis, preferred_element_type=jnp.float32)

    return jax.shard_map(local_fn, mesh=mesh, in_specs=(row_spec, row_spec, P(None), P(None)), out_specs=row_spec, check_vma=False)
```

profile of v0, /device:TPU:22, one launch (start us, length us, event | category | flops | bytes accessed | tf_op | source)
XLA Modules:
  0.0 409.1 jit_solution(11593533970705436559)
XLA Ops:
  0.0 6.8 %collective-permute-start.3 = (bf16[2048,512]{1,0:T(8,128)(2,1)}, bf16[2048,512]{1,0:T(8,128)(2,1)}, u32[]{:S(2)}, u32[]{:S(2)}) collective-permute-start(bf16[2048,512]{1,0:T(8,128)(2,1)} %param.6), channel_id=1, source_target_pairs={{0,15},{1,0},{2,1},{3,2},{4,3},{5,4},{6,5},{7,6},{8,7},{9,8},{10,9... | collective-permute-start | bytes 6291464 | tf_op jit(solution)/shard_map/ppermute | solution.py:45
  9.5 12.5 %multiply_subtract_fusion = f32[2048,2048]{0,1:T(8,128)} fusion(bf16[2048,512]{1,0:T(8,128)(2,1)} %param.6, f32[2048]{0:T(1024)S(1)} %multiply_reduce_fusion.3), kind=kOutput, calls=%fused_computation.12 | convolution fusion | flops 4307550208 | bytes 18882560 | tf_op jit(solution)/shard_map/nd,md->nm/dot_general | solution.py:12
  22.0 17.6 %copy.5 = f32[2048,2048]{1,0:T(8,128)} copy(f32[2048,2048]{0,1:T(8,128)} %multiply_subtract_fusion) | data formatting | bytes 33554432 | tf_op jit(solution)/shard_map/sub | solution.py:13
  40.9 7.7 %fusion.9 = f32[2048,16]{0,1:T(8,128)S(1)} fusion(bf16[2048,16]{0,1:T(8,128)(2,1)} %param.7, f32[2048,2048]{1,0:T(8,128)} %copy.5, f32[]{:T(128)} %bitcast.1, f32[]{:T(128)} %bitcast.50), kind=kOutput, calls=%fused_computation.19 | convolution fusion | flops 155189248 | bytes 16973832 | tf_op jit(solution)/shard_map/dot_general | solution.py:44
  50.6 6.9 %broadcast_add_fusion.1 = f32[2048,2048]{0,1:T(8,128)} fusion(f32[2048]{0:T(1024)S(1)} %multiply_reduce_fusion.2, f32[2048]{0:T(1024)S(1)} %multiply_reduce_fusion.3), kind=kLoop, calls=%fused_computation.15 | loop fusion | flops 4194304 | bytes 16793600 | tf_op jit(solution)/shard_map/add | solution.py:13
  57.5 17.6 %copy.7 = f32[2048,2048]{1,0:T(8,128)} copy(f32[2048,2048]{0,1:T(8,128)} %broadcast_add_fusion.1) | data formatting | bytes 33554432 | tf_op jit(solution)/shard_map/add | solution.py:13
  75.1 11.5 %multiply_convert_fusion.1 = bf16[2048,2048]{1,0:T(8,128)(2,1)S(1)} fusion(f32[2048,2048]{1,0:T(8,128)} %copy.7, bf16[2048,512]{1,0:T(8,128)(2,1)} %param.6, bf16[2048,512]{1,0:T(8,128)(2,1)} %collective-permute-done.3, f32[]{:T(128)} %bitcast.1, f32[]{:T(128)} %bitcast.52), kind=kOutput, calls=%fused_computation.10 | convolution fusion | flops 4324327424 | bytes 29360136 | tf_op jit(solution)/shard_map/nd,md->nm/dot_general | solution.py:12
  88.6 2.3 convolution_add_fusion.2
  90.9 251.1 %while.16 = (s32[]{:T(128)}, bf16[2048,512]{1,0:T(8,128)(2,1)}, bf16[2048,16]{0,1:T(8,128)(2,1)S(1)}, f32[2048,16]{0,1:T(8,128)S(1)}, f32[2048,16]{0,1:T(8,128)S...) while((s32[]{:T(128)}, bf16[2048,512]{1,0:T(8,128)(2,1)}, ...), condition=%wide.region_4.0_spmd, body=%wide.region_2.0_spmd.sunk | while | flops 4600166400 | bytes 45637868 | solution.py:48
  92.3 23.3 %collective-permute-done.1 = bf16[2048,16]{0,1:T(8,128)(2,1)S(1)} collective-permute-done((bf16[2048,16]{0,1:T(8,128)(2,1)S(1)}, bf16[2048,16]{0,1:T(8,128)(2,1)S(1)}, u32[]{:S(2)}, u32[]{:S(2)}) %collective-permute-start.1) | collective-permute-done | bytes 65568 | tf_op jit(solution)/shard_map/while/body/eval_jaxpr/ppermute | solution.py:38
  116.1 8.8 %multiply_convert_fusion.5 = bf16[2048,2048]{1,0:T(8,128)(2,1)S(1)} fusion(bf16[2048,512]{1,0:T(8,128)(2,1)} %get-tuple-element.174, bf16[2048,512]{1,0:T(8,128)(2,1)S(1)} %collective-permute-done, f32[]{:T(128)} %get-tuple-element.175, f32[2048]{0:T(1024)S(1)} %multiply_reduce_fusion.5, f32[2048]{0:T(1024)S(1)} %get-tuple-element.173, ...), kind=kOutput, calls=%fused_computation.clone.1 | convolution fusion | flops 4328521728 | bytes 12599304 | tf_op jit(solution)/shard_map/while/body/eval_jaxpr/nd,md->nm/dot_general | solution.py:12
  124.9 2.3 convolution_add_fusion.5
  130.5 3.2 collective-permute-start
  133.8 24.1 %collective-permute-done.1 = bf16[2048,16]{0,1:T(8,128)(2,1)S(1)} collective-permute-done((bf16[2048,16]{0,1:T(8,128)(2,1)S(1)}, bf16[2048,16]{0,1:T(8,128)(2,1)S(1)}, u32[]{:S(2)}, u32[]{:S(2)}) %collective-permute-start.1) | collective-permute-done | bytes 65568 | tf_op jit(solution)/shard_map/while/body/eval_jaxpr/ppermute | solution.py:38
  158.4 8.8 %multiply_convert_fusion.5 = bf16[2048,2048]{1,0:T(8,128)(2,1)S(1)} fusion(bf16[2048,512]{1,0:T(8,128)(2,1)} %get-tuple-element.174, bf16[2048,512]{1,0:T(8,128)(2,1)S(1)} %collective-permute-done, f32[]{:T(128)} %get-tuple-element.175, f32[2048]{0:T(1024)S(1)} %multiply_reduce_fusion.5, f32[2048]{0:T(1024)S(1)} %get-tuple-element.173, ...), kind=kOutput, calls=%fused_computation.clone.1 | convolution fusion | flops 4328521728 | bytes 12599304 | tf_op jit(solution)/shard_map/while/body/eval_jaxpr/nd,md->nm/dot_general | solution.py:12
  172.8 3.1 collective-permute-start
  176.1 24.1 %collective-permute-done.1 = bf16[2048,16]{0,1:T(8,128)(2,1)S(1)} collective-permute-done((bf16[2048,16]{0,1:T(8,128)(2,1)S(1)}, bf16[2048,16]{0,1:T(8,128)(2,1)S(1)}, u32[]{:S(2)}, u32[]{:S(2)}) %collective-permute-start.1) | collective-permute-done | bytes 65568 | tf_op jit(solution)/shard_map/while/body/eval_jaxpr/ppermute | solution.py:38
  200.7 8.8 %multiply_convert_fusion.5 = bf16[2048,2048]{1,0:T(8,128)(2,1)S(1)} fusion(bf16[2048,512]{1,0:T(8,128)(2,1)} %get-tuple-element.174, bf16[2048,512]{1,0:T(8,128)(2,1)S(1)} %collective-permute-done, f32[]{:T(128)} %get-tuple-element.175, f32[2048]{0:T(1024)S(1)} %multiply_reduce_fusion.5, f32[2048]{0:T(1024)S(1)} %get-tuple-element.173, ...), kind=kOutput, calls=%fused_computation.clone.1 | convolution fusion | flops 4328521728 | bytes 12599304 | tf_op jit(solution)/shard_map/while/body/eval_jaxpr/nd,md->nm/dot_general | solution.py:12
  215.1 3.1 collective-permute-start
  218.4 24.1 %collective-permute-done.1 = bf16[2048,16]{0,1:T(8,128)(2,1)S(1)} collective-permute-done((bf16[2048,16]{0,1:T(8,128)(2,1)S(1)}, bf16[2048,16]{0,1:T(8,128)(2,1)S(1)}, u32[]{:S(2)}, u32[]{:S(2)}) %collective-permute-start.1) | collective-permute-done | bytes 65568 | tf_op jit(solution)/shard_map/while/body/eval_jaxpr/ppermute | solution.py:38
  243.0 8.8 %multiply_convert_fusion.5 = bf16[2048,2048]{1,0:T(8,128)(2,1)S(1)} fusion(bf16[2048,512]{1,0:T(8,128)(2,1)} %get-tuple-element.174, bf16[2048,512]{1,0:T(8,128)(2,1)S(1)} %collective-permute-done, f32[]{:T(128)} %get-tuple-element.175, f32[2048]{0:T(1024)S(1)} %multiply_reduce_fusion.5, f32[2048]{0:T(1024)S(1)} %get-tuple-element.173, ...), kind=kOutput, calls=%fused_computation.clone.1 | convolution fusion | flops 4328521728 | bytes 12599304 | tf_op jit(solution)/shard_map/while/body/eval_jaxpr/nd,md->nm/dot_general | solution.py:12
  257.4 3.1 collective-permute-start
  260.7 24.1 %collective-permute-done.1 = bf16[2048,16]{0,1:T(8,128)(2,1)S(1)} collective-permute-done((bf16[2048,16]{0,1:T(8,128)(2,1)S(1)}, bf16[2048,16]{0,1:T(8,128)(2,1)S(1)}, u32[]{:S(2)}, u32[]{:S(2)}) %collective-permute-start.1) | collective-permute-done | bytes 65568 | tf_op jit(solution)/shard_map/while/body/eval_jaxpr/ppermute | solution.py:38
  285.3 8.8 %multiply_convert_fusion.5 = bf16[2048,2048]{1,0:T(8,128)(2,1)S(1)} fusion(bf16[2048,512]{1,0:T(8,128)(2,1)} %get-tuple-element.174, bf16[2048,512]{1,0:T(8,128)(2,1)S(1)} %collective-permute-done, f32[]{:T(128)} %get-tuple-element.175, f32[2048]{0:T(1024)S(1)} %multiply_reduce_fusion.5, f32[2048]{0:T(1024)S(1)} %get-tuple-element.173, ...), kind=kOutput, calls=%fused_computation.clone.1 | convolution fusion | flops 4328521728 | bytes 12599304 | tf_op jit(solution)/shard_map/while/body/eval_jaxpr/nd,md->nm/dot_general | solution.py:12
  299.7 3.1 collective-permute-start
  303.0 24.1 %collective-permute-done.1 = bf16[2048,16]{0,1:T(8,128)(2,1)S(1)} collective-permute-done((bf16[2048,16]{0,1:T(8,128)(2,1)S(1)}, bf16[2048,16]{0,1:T(8,128)(2,1)S(1)}, u32[]{:S(2)}, u32[]{:S(2)}) %collective-permute-start.1) | collective-permute-done | bytes 65568 | tf_op jit(solution)/shard_map/while/body/eval_jaxpr/ppermute | solution.py:38
  327.6 8.8 %multiply_convert_fusion.5 = bf16[2048,2048]{1,0:T(8,128)(2,1)S(1)} fusion(bf16[2048,512]{1,0:T(8,128)(2,1)} %get-tuple-element.174, bf16[2048,512]{1,0:T(8,128)(2,1)S(1)} %collective-permute-done, f32[]{:T(128)} %get-tuple-element.175, f32[2048]{0:T(1024)S(1)} %multiply_reduce_fusion.5, f32[2048]{0:T(1024)S(1)} %get-tuple-element.173, ...), kind=kOutput, calls=%fused_computation.clone.1 | convolution fusion | flops 4328521728 | bytes 12599304 | tf_op jit(solution)/shard_map/while/body/eval_jaxpr/nd,md->nm/dot_general | solution.py:12
  342.0 3.1 collective-permute-start.6
  345.3 23.8 %collective-permute-done.6 = bf16[2048,512]{1,0:T(8,128)(2,1)S(1)} collective-permute-done((bf16[2048,512]{1,0:T(8,128)(2,1)}, bf16[2048,512]{1,0:T(8,128)(2,1)S(1)}, u32[]{:S(2)}, u32[]{:S(2)}) %collective-permute-start.6) | collective-permute-done | bytes 2097184 | tf_op jit(solution)/shard_map/ppermute | solution.py:50
  369.5 6.9 %broadcast_add_fusion = f32[2048,2048]{0,1:T(8,128)} fusion(f32[2048]{0:T(1024)S(1)} %multiply_reduce_fusion.1, f32[2048]{0:T(1024)S(1)} %get-tuple-element.184), kind=kLoop, calls=%fused_computation.14 | loop fusion | flops 4194304 | bytes 16793600 | tf_op jit(solution)/shard_map/add | solution.py:13
  376.4 17.6 %copy.8 = f32[2048,2048]{1,0:T(8,128)} copy(f32[2048,2048]{0,1:T(8,128)} %broadcast_add_fusion) | data formatting | bytes 33554432 | tf_op jit(solution)/shard_map/add | solution.py:13
  394.0 15.1 %add_add_fusion = f32[2048,16]{0,1:T(8,128)} fusion(f32[2048,16]{0,1:T(8,128)S(1)} %get-tuple-element.60, f32[2048,16]{0,1:T(8,128)S(1)} %collective-permute-done.5, bf16[2048,16]{0,1:T(8,128)(2,1)S(1)} %collective-permute-done.7, f32[2048,2048]{1,0:T(8,128)} %copy.8, bf16[2048,512]{1,0:T(8,128)(2,1)S(1)} %collective-permute-done.6, ...), kind=kOutput, calls=%fused_computation.24 | convolution fusion | flops 4458610688 | bytes 21430280 | tf_op jit(solution)/shard_map/dot_general | solution.py:53
  (65 shorter events, 43.7 us)
Async XLA Ops:
  0.0 48.6 %collective-permute-start.3 = (bf16[2048,512]{1,0:T(8,128)(2,1)}, bf16[2048,512]{1,0:T(8,128)(2,1)}, u32[]{:S(2)}, u32[]{:S(2)}) collective-permute-start(bf16[2048,512]{1,0:T(8,128)(2,1)} %param.6), channel_id=1, source_target_pairs={{0,15},{1,0},{2,1},{3,2},{4,3},{5,4},{6,5},{7,6},{8,7},{9,8},{10,9... | collective-permute-start | bytes 6291464 | tf_op jit(solution)/shard_map/ppermute | solution.py:45
  6.8 81.8 %collective-permute-start.4 = (bf16[2048,16]{0,1:T(8,128)(2,1)}, bf16[2048,16]{0,1:T(8,128)(2,1)S(1)}, u32[]{:S(2)}, u32[]{:S(2)}) collective-permute-start(bf16[2048,16]{0,1:T(8,128)(2,1)} %param.7), channel_id=1, source_target_pairs={{0,15},{1,0},{2,1},{3,2},{4,3},{5,4},{6,5},{7,6},{8,7},{9,8},{10,9... | collective-permute-start | bytes 196616 | tf_op jit(solution)/shard_map/ppermute | solution.py:46
  91.0 24.6 %collective-permute-start = (bf16[2048,512]{1,0:T(8,128)(2,1)}, bf16[2048,512]{1,0:T(8,128)(2,1)S(1)}, u32[]{:S(2)}, u32[]{:S(2)}) collective-permute-start(bf16[2048,512]{1,0:T(8,128)(2,1)} %get-tuple-element.157), channel_id=1, source_target_pairs={{0,15},{1,0},{2,1},{3,2},{4,3},{5,4},{6,5},{7,6},{8,7},{9,8},{10,9... | collective-permute-start | bytes 6291464 | tf_op jit(solution)/shard_map/while/body/eval_jaxpr/ppermute | solution.py:37
  91.4 24.2 %collective-permute-start.1 = (bf16[2048,16]{0,1:T(8,128)(2,1)S(1)}, bf16[2048,16]{0,1:T(8,128)(2,1)S(1)}, u32[]{:S(2)}, u32[]{:S(2)}) collective-permute-start(bf16[2048,16]{0,1:T(8,128)(2,1)S(1)} %get-tuple-element.158), channel_id=1, source_target_pairs={{0,15},{1,0},{2,1},{3,2},{4,3},{5,4},{6,5},{7,6},{8,7},{9,8},{10,9... | collective-permute-start | bytes 196616 | tf_op jit(solution)/shard_map/while/body/eval_jaxpr/ppermute | solution.py:38
  92.0 36.5 %collective-permute-start.2 = (f32[2048,16]{0,1:T(8,128)S(1)}, f32[2048,16]{0,1:T(8,128)S(1)}, u32[]{:S(2)}, u32[]{:S(2)}) collective-permute-start(f32[2048,16]{0,1:T(8,128)S(1)} %get-tuple-element.160), channel_id=1, source_target_pairs={{0,15},{1,0},{2,1},{3,2},{4,3},{5,4},{6,5},{7,6},{8,7},{9,8},{10,9... | collective-permute-start | bytes 393224 | tf_op jit(solution)/shard_map/while/body/eval_jaxpr/ppermute | solution.py:39
  130.5 27.4 %collective-permute-start = (bf16[2048,512]{1,0:T(8,128)(2,1)}, bf16[2048,512]{1,0:T(8,128)(2,1)S(1)}, u32[]{:S(2)}, u32[]{:S(2)}) collective-permute-start(bf16[2048,512]{1,0:T(8,128)(2,1)} %get-tuple-element.157), channel_id=1, source_target_pairs={{0,15},{1,0},{2,1},{3,2},{4,3},{5,4},{6,5},{7,6},{8,7},{9,8},{10,9... | collective-permute-start | bytes 6291464 | tf_op jit(solution)/shard_map/while/body/eval_jaxpr/ppermute | solution.py:37
  133.7 24.2 %collective-permute-start.1 = (bf16[2048,16]{0,1:T(8,128)(2,1)S(1)}, bf16[2048,16]{0,1:T(8,128)(2,1)S(1)}, u32[]{:S(2)}, u32[]{:S(2)}) collective-permute-start(bf16[2048,16]{0,1:T(8,128)(2,1)S(1)} %get-tuple-element.158), channel_id=1, source_target_pairs={{0,15},{1,0},{2,1},{3,2},{4,3},{5,4},{6,5},{7,6},{8,7},{9,8},{10,9... | collective-permute-start | bytes 196616 | tf_op jit(solution)/shard_map/while/body/eval_jaxpr/ppermute | solution.py:38
  133.7 37.1 %collective-permute-start.2 = (f32[2048,16]{0,1:T(8,128)S(1)}, f32[2048,16]{0,1:T(8,128)S(1)}, u32[]{:S(2)}, u32[]{:S(2)}) collective-permute-start(f32[2048,16]{0,1:T(8,128)S(1)} %get-tuple-element.160), channel_id=1, source_target_pairs={{0,15},{1,0},{2,1},{3,2},{4,3},{5,4},{6,5},{7,6},{8,7},{9,8},{10,9... | collective-permute-start | bytes 393224 | tf_op jit(solution)/shard_map/while/body/eval_jaxpr/ppermute | solution.py:39
  172.8 27.4 %collective-permute-start = (bf16[2048,512]{1,0:T(8,128)(2,1)}, bf16[2048,512]{1,0:T(8,128)(2,1)S(1)}, u32[]{:S(2)}, u32[]{:S(2)}) collective-permute-start(bf16[2048,512]{1,0:T(8,128)(2,1)} %get-tuple-element.157), channel_id=1, source_target_pairs={{0,15},{1,0},{2,1},{3,2},{4,3},{5,4},{6,5},{7,6},{8,7},{9,8},{10,9... | collective-permute-start | bytes 6291464 | tf_op jit(solution)/shard_map/while/body/eval_jaxpr/ppermute | solution.py:37
  176.0 24.2 %collective-permute-start.1 = (bf16[2048,16]{0,1:T(8,128)(2,1)S(1)}, bf16[2048,16]{0,1:T(8,128)(2,1)S(1)}, u32[]{:S(2)}, u32[]{:S(2)}) collective-permute-start(bf16[2048,16]{0,1:T(8,128)(2,1)S(1)} %get-tuple-element.158), channel_id=1, source_target_pairs={{0,15},{1,0},{2,1},{3,2},{4,3},{5,4},{6,5},{7,6},{8,7},{9,8},{10,9... | collective-permute-start | bytes 196616 | tf_op jit(solution)/shard_map/while/body/eval_jaxpr/ppermute | solution.py:38
  176.0 37.1 %collective-permute-start.2 = (f32[2048,16]{0,1:T(8,128)S(1)}, f32[2048,16]{0,1:T(8,128)S(1)}, u32[]{:S(2)}, u32[]{:S(2)}) collective-permute-start(f32[2048,16]{0,1:T(8,128)S(1)} %get-tuple-element.160), channel_id=1, source_target_pairs={{0,15},{1,0},{2,1},{3,2},{4,3},{5,4},{6,5},{7,6},{8,7},{9,8},{10,9... | collective-permute-start | bytes 393224 | tf_op jit(solution)/shard_map/while/body/eval_jaxpr/ppermute | solution.py:39
  215.1 27.4 %collective-permute-start = (bf16[2048,512]{1,0:T(8,128)(2,1)}, bf16[2048,512]{1,0:T(8,128)(2,1)S(1)}, u32[]{:S(2)}, u32[]{:S(2)}) collective-permute-start(bf16[2048,512]{1,0:T(8,128)(2,1)} %get-tuple-element.157), channel_id=1, source_target_pairs={{0,15},{1,0},{2,1},{3,2},{4,3},{5,4},{6,5},{7,6},{8,7},{9,8},{10,9... | collective-permute-start | bytes 6291464 | tf_op jit(solution)/shard_map/while/body/eval_jaxpr/ppermute | solution.py:37
  218.3 24.2 %collective-permute-start.1 = (bf16[2048,16]{0,1:T(8,128)(2,1)S(1)}, bf16[2048,16]{0,1:T(8,128)(2,1)S(1)}, u32[]{:S(2)}, u32[]{:S(2)}) collective-permute-start(bf16[2048,16]{0,1:T(8,128)(2,1)S(1)} %get-tuple-element.158), channel_id=1, source_target_pairs={{0,15},{1,0},{2,1},{3,2},{4,3},{5,4},{6,5},{7,6},{8,7},{9,8},{10,9... | collective-permute-start | bytes 196616 | tf_op jit(solution)/shard_map/while/body/eval_jaxpr/ppermute | solution.py:38
  218.3 37.1 %collective-permute-start.2 = (f32[2048,16]{0,1:T(8,128)S(1)}, f32[2048,16]{0,1:T(8,128)S(1)}, u32[]{:S(2)}, u32[]{:S(2)}) collective-permute-start(f32[2048,16]{0,1:T(8,128)S(1)} %get-tuple-element.160), channel_id=1, source_target_pairs={{0,15},{1,0},{2,1},{3,2},{4,3},{5,4},{6,5},{7,6},{8,7},{9,8},{10,9... | collective-permute-start | bytes 393224 | tf_op jit(solution)/shard_map/while/body/eval_jaxpr/ppermute | solution.py:39
  257.4 27.4 %collective-permute-start = (bf16[2048,512]{1,0:T(8,128)(2,1)}, bf16[2048,512]{1,0:T(8,128)(2,1)S(1)}, u32[]{:S(2)}, u32[]{:S(2)}) collective-permute-start(bf16[2048,512]{1,0:T(8,128)(2,1)} %get-tuple-element.157), channel_id=1, source_target_pairs={{0,15},{1,0},{2,1},{3,2},{4,3},{5,4},{6,5},{7,6},{8,7},{9,8},{10,9... | collective-permute-start | bytes 6291464 | tf_op jit(solution)/shard_map/while/body/eval_jaxpr/ppermute | solution.py:37
  260.6 24.2 %collective-permute-start.1 = (bf16[2048,16]{0,1:T(8,128)(2,1)S(1)}, bf16[2048,16]{0,1:T(8,128)(2,1)S(1)}, u32[]{:S(2)}, u32[]{:S(2)}) collective-permute-start(bf16[2048,16]{0,1:T(8,128)(2,1)S(1)} %get-tuple-element.158), channel_id=1, source_target_pairs={{0,15},{1,0},{2,1},{3,2},{4,3},{5,4},{6,5},{7,6},{8,7},{9,8},{10,9... | collective-permute-start | bytes 196616 | tf_op jit(solution)/shard_map/while/body/eval_jaxpr/ppermute | solution.py:38
  260.6 37.1 %collective-permute-start.2 = (f32[2048,16]{0,1:T(8,128)S(1)}, f32[2048,16]{0,1:T(8,128)S(1)}, u32[]{:S(2)}, u32[]{:S(2)}) collective-permute-start(f32[2048,16]{0,1:T(8,128)S(1)} %get-tuple-element.160), channel_id=1, source_target_pairs={{0,15},{1,0},{2,1},{3,2},{4,3},{5,4},{6,5},{7,6},{8,7},{9,8},{10,9... | collective-permute-start | bytes 393224 | tf_op jit(solution)/shard_map/while/body/eval_jaxpr/ppermute | solution.py:39
  299.7 27.4 %collective-permute-start = (bf16[2048,512]{1,0:T(8,128)(2,1)}, bf16[2048,512]{1,0:T(8,128)(2,1)S(1)}, u32[]{:S(2)}, u32[]{:S(2)}) collective-permute-start(bf16[2048,512]{1,0:T(8,128)(2,1)} %get-tuple-element.157), channel_id=1, source_target_pairs={{0,15},{1,0},{2,1},{3,2},{4,3},{5,4},{6,5},{7,6},{8,7},{9,8},{10,9... | collective-permute-start | bytes 6291464 | tf_op jit(solution)/shard_map/while/body/eval_jaxpr/ppermute | solution.py:37
  302.9 24.2 %collective-permute-start.1 = (bf16[2048,16]{0,1:T(8,128)(2,1)S(1)}, bf16[2048,16]{0,1:T(8,128)(2,1)S(1)}, u32[]{:S(2)}, u32[]{:S(2)}) collective-permute-start(bf16[2048,16]{0,1:T(8,128)(2,1)S(1)} %get-tuple-element.158), channel_id=1, source_target_pairs={{0,15},{1,0},{2,1},{3,2},{4,3},{5,4},{6,5},{7,6},{8,7},{9,8},{10,9... | collective-permute-start | bytes 196616 | tf_op jit(solution)/shard_map/while/body/eval_jaxpr/ppermute | solution.py:38
  302.9 37.1 %collective-permute-start.2 = (f32[2048,16]{0,1:T(8,128)S(1)}, f32[2048,16]{0,1:T(8,128)S(1)}, u32[]{:S(2)}, u32[]{:S(2)}) collective-permute-start(f32[2048,16]{0,1:T(8,128)S(1)} %get-tuple-element.160), channel_id=1, source_target_pairs={{0,15},{1,0},{2,1},{3,2},{4,3},{5,4},{6,5},{7,6},{8,7},{9,8},{10,9... | collective-permute-start | bytes 393224 | tf_op jit(solution)/shard_map/while/body/eval_jaxpr/ppermute | solution.py:39
  342.0 27.0 %collective-permute-start.6 = (bf16[2048,512]{1,0:T(8,128)(2,1)}, bf16[2048,512]{1,0:T(8,128)(2,1)S(1)}, u32[]{:S(2)}, u32[]{:S(2)}) collective-permute-start(bf16[2048,512]{1,0:T(8,128)(2,1)} %get-tuple-element.62), channel_id=1, source_target_pairs={{0,15},{1,0},{2,1},{3,2},{4,3},{5,4},{6,5},{7,6},{8,7},{9,8},{10,9... | collective-permute-start | bytes 6291464 | tf_op jit(solution)/shard_map/ppermute | solution.py:50
  345.1 48.8 %collective-permute-start.5 = (f32[2048,16]{0,1:T(8,128)S(1)}, f32[2048,16]{0,1:T(8,128)S(1)}, u32[]{:S(2)}, u32[]{:S(2)}) collective-permute-start(f32[2048,16]{0,1:T(8,128)S(1)} %get-tuple-element.61), channel_id=1, source_target_pairs={{0,7},{1,8},{2,9},{3,10},{4,11},{5,12},{6,13},{7,14},{8,15},{9,0},... | collective-permute-start | bytes 393224 | tf_op jit(solution)/shard_map/ppermute | solution.py:49
  345.1 48.8 %collective-permute-start.7 = (bf16[2048,16]{0,1:T(8,128)(2,1)S(1)}, bf16[2048,16]{0,1:T(8,128)(2,1)S(1)}, u32[]{:S(2)}, u32[]{:S(2)}) collective-permute-start(bf16[2048,16]{0,1:T(8,128)(2,1)S(1)} %get-tuple-element.63), channel_id=1, source_target_pairs={{0,15},{1,0},{2,1},{3,2},{4,3},{5,4},{6,5},{7,6},{8,7},{9,8},{10,9... | collective-permute-start | bytes 196616 | tf_op jit(solution)/shard_map/ppermute | solution.py:51
where the time goes:
time: 410 us; the launch traced here: 409 us
  waiting for transfers between devices  168 us (41%)
  matrix products  130 us (32%)
  local copies, waits for them, and re-layouts  60.8 us (15%)
  starting transfers between devices  28.1 us (7%)
  other arithmetic  21.2 us (5%)
    ppermute x6, waiting for transfers between devices, loop_body(): v_vis = lax.ppermute(v_vis, 'group', shift_left)  144 us
    dot_general x8, matrix products, kernel_block(): jnp.einsum('nd,md->nm', x_rows, x_cols, preferred_element_type=jnp.float32)  76.6 us
    add x2, local copies, waits for them, and re-layouts, kernel_block(): norm_rows[:, None] + norm_cols[None, :] - 2.0 * gram_mat  35.2 us
    ppermute x1, waiting for transfers between devices, local_fn(): x_vis = lax.ppermute(x_vis, 'group', shift_left)  23.8 us
    sub x1, local copies, waits for them, and re-layouts, kernel_block(): norm_rows[:, None] + norm_cols[None, :] - 2.0 * gram_mat  17.6 us
    ppermute x6, starting transfers between devices, loop_body(): x_vis = lax.ppermute(x_vis, 'group', shift_left)  16.1 us
    dot_general x7, matrix products, pair_step(): jnp.dot(kern_pair, v_vis, preferred_element_type=jnp.float32)  15.9 us
    dot_general x1, matrix products, local_fn(): return y_acc + jnp.dot(kern_far, v_vis, preferred_element_type=jnp.float32)  15.1 us
  transfers between devices with their start and end apart: 23, of which 7 were waited for; matrix products, arithmetic and copies ran while one was open for 44% of the time, Pallas kernels for 0%

commit v1 on v0

v1 whole, which is shorter than its diff:
```python
import jax
import jax.numpy as jnp
from jax import lax
from jax.experimental import pallas as pl
from jax.experimental.pallas import tpu as pltpu
from jax.sharding import PartitionSpec as P

MESH = pl.DeviceIdType.MESH
NT = (((1,), (1,)), ((), ()))
NN = (((1,), (0,)), ((), ()))
LOG2E = 1.4426950408889634
M2, M1, OWN, P1, P2, T0, T1, TF = range(8)
R_OWN, R_T0, R_M1, R_P1, R_T1, R_FAR = range(6)
C_M1, C_P1, C_M2, C_P2, C_T1, C_TF, C_T0 = range(7)
N_CHUNK = 8
ROWS = 1024


def dot(a, b, dims):
    return lax.dot_general(a, b, dims, preferred_element_type=jnp.float32)


def kernel(n_group, ell_ref, s_ref, x_ref, v_ref, y_ref, xs, vt, nrm, arep, acc, rx,
           load_sem, x_send, x_recv, v_send, v_recv, n_send, n_recv, t0_sem, r_send, r_recv):
    n_rows = x_ref.shape[0]
    chunk = n_rows // N_CHUNK
    n_chip = n_group // 2
    me = lax.axis_index('group')
    chip, core = me // 2, me % 2
    up = ((chip + 1) % n_chip) * 2 + core
    down = ((chip + n_chip - 1) % n_chip) * 2 + core
    partner = chip * 2 + 1 - core
    far_half = chip // (n_chip // 2)
    far_row = M2 + (P2 - M2) * far_half
    far_col = P2 - (P2 - M2) * far_half
    far_base = pl.multiple_of(far_half * ROWS, ROWS)

    def rows_of(j):
        return pl.ds(pl.multiple_of(j * chunk, chunk), chunk)

    def flip(j):
        return (j + N_CHUNK // 2) % N_CHUNK

    SRC = {C_M1: OWN, C_P1: OWN, C_M2: M1, C_P2: P1, C_T1: P1, C_TF: far_col, C_T0: OWN}
    DST = {C_M1: M1, C_P1: P1, C_M2: M2, C_P2: P2, C_T1: T1, C_TF: TF, C_T0: T0}
    TO = {C_M1: up, C_P1: down, C_M2: up, C_P2: down, C_T1: partner, C_TF: partner, C_T0: partner}

    def x_copy(c, j):
        return pltpu.make_async_remote_copy(
            src_ref=xs.at[SRC[c], rows_of(j)], dst_ref=xs.at[DST[c], rows_of(j)],
            send_sem=x_send.at[c, j], recv_sem=x_recv.at[c, j],
            device_id={'group': TO[c]}, device_id_type=MESH)

    def t0_copy():
        return pltpu.make_async_remote_copy(
            src_ref=xs.at[OWN], dst_ref=xs.at[T0], send_sem=t0_sem.at[0], recv_sem=t0_sem.at[1],
            device_id={'group': partner}, device_id_type=MESH)

    def v_copy(c):
        src = v_ref if c in (C_M1, C_P1, C_T0) else vt.at[SRC[c]]
        return pltpu.make_async_remote_copy(
            src_ref=src, dst_ref=vt.at[DST[c]], send_sem=v_send.at[c], recv_sem=v_recv.at[c],
            device_id={'group': TO[c]}, device_id_type=MESH)

    def n_copy(c):
        return pltpu.make_async_remote_copy(
            src_ref=nrm.at[SRC[c]], dst_ref=nrm.at[DST[c]], send_sem=n_send.at[c], recv_sem=n_recv.at[c],
            device_id={'group': TO[c]}, device_id_type=MESH)

    def r_copy(src, i, to):
        return pltpu.make_async_remote_copy(
            src_ref=acc.at[src], dst_ref=rx.at[i], send_sem=r_send.at[i], recv_sem=r_recv.at[i],
            device_id={'group': to}, device_id_type=MESH)

    def load(j):
        return pltpu.make_async_copy(x_ref.at[rows_of(j)], xs.at[OWN, rows_of(j)], load_sem.at[j])

    for j in range(N_CHUNK):
        load(j).start()
    barrier = pltpu.get_barrier_semaphore()
    for peer in (up, down, partner):
        pl.semaphore_signal(barrier, inc=1, device_id={'group': peer}, device_id_type=MESH)
    pl.semaphore_wait(barrier, 3)
    for c in (C_M1, C_P1, C_T0):
        v_copy(c).start()
    for j in range(N_CHUNK):
        load(j).wait()
    for j in range(N_CHUNK):
        x_copy(C_M1, j).start()
        x_copy(C_P1, flip(j)).start()
    t0_copy().start()

    ell = jnp.full((1, 128), ell_ref[0], jnp.float32)
    coef = LOG2E / (2.0 * jnp.square(ell))
    top = LOG2E * jnp.log(jnp.full((1, 128), s_ref[0], jnp.float32))
    coef_2 = jnp.concatenate([coef, coef], axis=1)
    two_coef = 2.0 * coef_2
    top_2 = jnp.concatenate([top, top], axis=1)

    acc[...] = jnp.zeros_like(acc)
    vt[OWN] = v_ref[...]

    def own_norms(b, _):
        rows = pl.ds(pl.multiple_of(b * 128, 128), 128)
        part = jnp.sum(jnp.square(xs[OWN, rows, :].astype(jnp.float32)), axis=1, keepdims=True)
        part = jnp.broadcast_to(part, (128, 128))
        arep[R_OWN, rows, :] = part * coef - top
        nrm[OWN, :, rows] = part.T[0:1, :]
        return 0

    lax.fori_loop(0, n_rows // 128, own_norms, 0)

    def column_norms(slot, to, start, n):
        def one(b, _):
            src = pl.ds(pl.multiple_of(start + b * 128, 128), 128)
            dst = pl.ds(pl.multiple_of(b * 128, 128), 128)
            row = jnp.broadcast_to(nrm[slot, :, src], (128, 128))
            arep[to, dst, :] = row.T * coef - top
            return 0
        lax.fori_loop(0, n // 128, one, 0)

    def unit(row_slot, row_start, rep_slot, rep_start, col_slot, j, want_row):
        rows = pl.ds(pl.multiple_of(row_start, ROWS), ROWS)
        reps = pl.ds(pl.multiple_of(rep_start, ROWS), ROWS)
        cols = rows_of(j)
        gram = dot(xs[row_slot, rows, :], xs[col_slot, cols, :], NT)
        shift = arep[rep_slot, reps, :]
        shift = jnp.concatenate([shift, shift], axis=1)
        expo = jnp.minimum(gram * two_coef - shift - nrm[col_slot, :, cols] * coef_2, top_2)
        kern = jnp.exp2(expo).astype(jnp.bfloat16)
        acc[col_slot, :, cols] += dot(vt[row_slot, :, rows], kern, NN)
        if want_row:
            acc[row_slot, :, rows] += dot(vt[col_slot, :, cols], kern, NT)

    def own_part(row_slot, rep_slot):
        def one(u, _):
            half, j = u // N_CHUNK, u % N_CHUNK
            start = half * ROWS
            rows = pl.ds(pl.multiple_of(start, ROWS), ROWS)
            cols = rows_of(j)
            gram = dot(xs[row_slot, rows, :], xs[OWN, cols, :], NT)
            shift = arep[rep_slot, rows, :]
            shift = jnp.concatenate([shift, shift], axis=1)
            expo = jnp.minimum(gram * two_coef - shift - nrm[OWN, :, cols] * coef_2, top_2)
            kern = jnp.exp2(expo).astype(jnp.bfloat16)
            acc[OWN, :, cols] += dot(vt[row_slot, :, rows], kern, NN)
            return 0
        lax.fori_loop(0, 2 * N_CHUNK, one, 0)

    own_part(OWN, R_OWN)
    for c in (C_M1, C_P1, C_T0):
        n_copy(c).start()
    v_copy(C_T0).wait_recv()
    n_copy(C_T0).wait_recv()
    t0_copy().wait_recv()
    column_norms(T0, R_T0, 0, n_rows)
    v_copy(C_M1).wait_recv()
    n_copy(C_M1).wait_recv()
    v_copy(C_P1).wait_recv()
    n_copy(C_P1).wait_recv()
    for c in (C_M2, C_P2, C_T1):
        v_copy(c).start()
        n_copy(c).start()
    own_part(T0, R_T0)
    column_norms(M1, R_M1, 0, n_rows)
    column_norms(P1, R_P1, 0, n_rows)
    v_copy(C_T1).wait_recv()
    n_copy(C_T1).wait_recv()
    column_norms(T1, R_T1, 0, n_rows)

    def near_step(j, _):
        k = flip(j)
        x_copy(C_P1, k).wait_recv()
        x_copy(C_T1, k).start()
        x_copy(C_P2, k).start()
        x_copy(C_M1, j).wait_recv()
        x_copy(C_M2, j).start()

        x_copy(C_T1, k).wait_recv()

        def one(h, _):
            unit(OWN, h * ROWS, R_OWN, h * ROWS, P1, k, True)
            unit(OWN, h * ROWS, R_OWN, h * ROWS, T1, k, True)
            return 0
        lax.fori_loop(0, 2, one, 0)

        lo = jnp.where(j < 3, 4, jnp.where(j == 3, 0, j))
        hi = jnp.where(j < 3, 4, j + 1)

        def two(i, _):
            unit(M1, 0, R_M1, 0, P1, flip(i), True)
            unit(M1, 0, R_M1, 0, T1, flip(i), True)
            return 0
        lax.fori_loop(lo, hi, two, 0)
        return 0

    lax.fori_loop(0, N_CHUNK, near_step, 0)

    def rest(i, _):
        unit(M1, ROWS, R_M1, ROWS, P1, i, True)
        unit(M1, ROWS, R_M1, ROWS, T1, i, True)
        return 0
    lax.fori_loop(0, N_CHUNK, rest, 0)

    v_copy(C_M2).wait_recv()
    n_copy(C_M2).wait_recv()
    v_copy(C_P2).wait_recv()
    n_copy(C_P2).wait_recv()
    v_copy(C_TF).start()
    n_copy(C_TF).start()
    column_norms(far_row, R_FAR, far_base, ROWS)
    v_copy(C_TF).wait_recv()
    n_copy(C_TF).wait_recv()

    def far_step(j, _):
        k = flip(j)
        m = jnp.where(far_half == 0, k, j)
        x_copy(C_M2, j).wait_recv()
        x_copy(C_P2, k).wait_recv()
        x_copy(C_TF, m).start()

        def one(h, _):
            unit(P1, h * ROWS, R_P1, h * ROWS, M2, j, True)
            unit(T1, h * ROWS, R_T1, h * ROWS, M2, j, True)
            return 0
        lax.fori_loop(0, 2, one, 0)
        x_copy(C_TF, m).wait_recv()

        lo = jnp.where(j < 3, 4, jnp.where(j == 3, 0, j))
        hi = jnp.where(j < 3, 4, j + 1)

        def two(i, _):
            q = jnp.where(far_half == 0, flip(i), i)
            unit(far_row, far_base, R_FAR, 0, far_col, q, True)
            unit_far(q)
            return 0

        def unit_far(q):
            rows = pl.ds(far_base, ROWS)
            cols = rows_of(q)
            gram = dot(xs[far_row, rows, :], xs[TF, cols, :], NT)
            shift = arep[R_FAR, 0:ROWS, :]
            shift = jnp.concatenate([shift, shift], axis=1)
            expo = jnp.minimum(gram * two_coef - shift - nrm[TF, :, cols] * coef_2, top_2)
            kern = jnp.exp2(expo).astype(jnp.bfloat16)
            acc[TF, :, cols] += dot(vt[far_row, :, rows], kern, NN)
            acc[far_row, :, rows] += dot(vt[TF, :, cols], kern, NT)
        lax.fori_loop(lo, hi, two, 0)
        return 0

    lax.fori_loop(0, N_CHUNK, far_step, 0)

    r_copy(T1, 0, partner).start()
    r_copy(TF, 1, partner).start()
    r_copy(TF, 1, partner).wait_recv()
    acc[far_col] += rx[1]
    r_copy(M2, 2, down).start()
    r_copy(P2, 3, up).start()
    r_copy(T1, 0, partner).wait_recv()
    acc[P1] += rx[0]
    r_copy(M2, 2, down).wait_recv()
    acc[M1] += rx[2]
    r_copy(M1, 4, down).start()
    r_copy(P2, 3, up).wait_recv()
    acc[P1] += rx[3]
    r_copy(P1, 5, up).start()
    r_copy(M1, 4, down).wait_recv()
    r_copy(P1, 5, up).wait_recv()
    y_ref[...] = acc[OWN] + rx[4] + rx[5]

    def drain(j, _):
        for c in (C_M1, C_P1, C_M2, C_P2, C_T1, C_TF):
            x_copy(c, j).wait_send()
        return 0
    lax.fori_loop(0, N_CHUNK, drain, 0)
    t0_copy().wait_send()
    for c in range(7):
        v_copy(c).wait_send()
        n_copy(c).wait_send()
    for i, (src, to) in enumerate(((T1, partner), (TF, partner), (M2, down), (P2, up), (M1, down), (P1, up))):
        r_copy(src, i, to).wait_send()


def solution(mesh):
    n_group = mesh.shape['group']
    row_spec = P(('tasks', 'group'), None)

    def local_fn(x_loc, v_loc, lengthscale, outscale):
        n_rows, n_feat = x_loc.shape
        n_rhs = v_loc.shape[1]
        smem = pl.BlockSpec(memory_space=pltpu.SMEM)
        vmem = pl.BlockSpec(memory_space=pltpu.VMEM)

        def body(*refs):
            kernel(n_group, *refs)

        y_t = pl.pallas_call(
            body,
            name='gauss_ring',
            out_shape=jax.ShapeDtypeStruct((n_rhs, n_rows), jnp.float32),
            in_specs=[smem, smem, pl.BlockSpec(memory_space=pl.ANY), vmem],
            out_specs=vmem,
            scratch_shapes=[
                pltpu.VMEM((8, n_rows, n_feat), jnp.bfloat16),
                pltpu.VMEM((8, n_rhs, n_rows), jnp.bfloat16),
                pltpu.VMEM((8, 1, n_rows), jnp.float32),
                pltpu.VMEM((6, n_rows, 128), jnp.float32),
                pltpu.VMEM((8, n_rhs, n_rows), jnp.float32),
                pltpu.VMEM((6, n_rhs, n_rows), jnp.float32),
                pltpu.SemaphoreType.DMA((N_CHUNK,)),
                pltpu.SemaphoreType.DMA((6, N_CHUNK)),
                pltpu.SemaphoreType.DMA((6, N_CHUNK)),
                pltpu.SemaphoreType.DMA((7,)),
                pltpu.SemaphoreType.DMA((7,)),
                pltpu.SemaphoreType.DMA((7,)),
                pltpu.SemaphoreType.DMA((7,)),
                pltpu.SemaphoreType.DMA((2,)),
                pltpu.SemaphoreType.DMA((6,)),
                pltpu.SemaphoreType.DMA((6,)),
            ],
            compiler_params=pltpu.CompilerParams(
                collective_id=0, has_side_effects=True, vmem_limit_bytes=56 * 2**20),
        )(lengthscale, outscale, x_loc, v_loc.T)
        return y_t.T

    return jax.shard_map(local_fn, mesh=mesh, in_specs=(row_spec, row_spec, P(None), P(None)), out_specs=row_spec, check_vma=False)
```

time: 410 us -> 221 us (0.54)
  Pallas kernels: 0 us -> 218 us
  waiting for transfers between devices: 168 us -> 0 us
  matrix products: 130 us -> 0 us
  local copies, waits for them, and re-layouts: 60.8 us -> 1.57 us
  starting transfers between devices: 28.1 us -> 0 us
  other arithmetic: 21.2 us -> 0 us
    pallas_call x0 -> x1, Pallas kernels: none -> 218 us  [local_fn(): pl.pallas_call(body, name='gauss_ring', out_shape=jax.ShapeDtypeStruct((n...]
    ppermute x23 -> x0, waiting for transfers between devices: 168 us -> none  [the longest x6 144 us: loop_body(): v_vis = lax.ppermute(v_vis, 'group', shift_left)]
    dot_general x24 -> x0, matrix products: 130 us -> none  [the longest x8 76.6 us: kernel_block(): jnp.einsum('nd,md->nm', x_rows, x_cols, preferred_element_type=jnp.float32)]
    add x2 -> x0, local copies, waits for them, and re-layouts: 35.2 us -> none  [kernel_block(): norm_rows[:, None] + norm_cols[None, :] - 2.0 * gram_mat]
    ppermute x23 -> x0, starting transfers between devices: 28.1 us -> none  [the longest x6 16.1 us: loop_body(): x_vis = lax.ppermute(x_vis, 'group', shift_left)]
    sub x1 -> x0, local copies, waits for them, and re-layouts: 17.6 us -> none  [kernel_block(): norm_rows[:, None] + norm_cols[None, :] - 2.0 * gram_mat]
    add x2 -> x0, other arithmetic: 13.7 us -> none  [kernel_block(): norm_rows[:, None] + norm_cols[None, :] - 2.0 * gram_mat]
    while x12 -> x0, local copies, waits for them, and re-layouts: 8.02 us -> none
  transfers between devices with their start and end apart: 23 -> 0, of which waited for: 7 -> 0; matrix products, arithmetic and copies ran while one was open for 44% -> 0% of each run, Pallas kernels for 0% -> 0%
where the time goes in v1:
time: 221 us
  Pallas kernels  218 us (99%)
    pallas_call x1, Pallas kernels, local_fn(): pl.pallas_call(body, name='gauss_ring', out_shape=jax.ShapeDtypeStruct((n...  218 us

profile of v1, /device:TPU:22, one launch (start us, length us, event | category | flops | bytes accessed | tf_op | source)
XLA Modules:
  0.0 221.1 jit_solution(9566644001370285697)
XLA Ops:
  1.3 218.2 %gauss_ring.1 = f32[16,2048]{1,0:T(8,128)} custom-call(f32[1]{0:T(128)S(6)} %copy.6.refs_0_, f32[1]{0:T(128)S(6)} %copy.7.refs_1_, bf16[2048,512]{1,0:T(8,128)(2,1)} %refs_2_.1, bf16[16,2048]{1,0:T(8,128)(2,1)} %bitcast.3), custom_call_target="tpu_custom_call" | custom-call | tf_op jit(solution)/shard_map/gauss_ring/pallas_call | solution.py:297
  219.5 1.6 copy.8

commit v2 on v1

v2 whole, which is shorter than its diff:
```python
import jax
import jax.numpy as jnp
from jax import lax
from jax.experimental import pallas as pl
from jax.experimental.pallas import tpu as pltpu
from jax.sharding import PartitionSpec as P

MESH = pl.DeviceIdType.MESH
LOG2E = 1.4426950408889634
M2, M1, OWN, P1, P2, T0, T1, T2, TM2 = range(9)
N_SLOT = 9
R_OWN, R_T0, R_P1, R_T1, R_P2, R_T2, R_FAR, R_TFAR = range(8)
N_REP = 8
NT = (((1,), (1,)), ((), ()))
NN = (((1,), (0,)), ((), ()))
C_M1, C_P1, C_M2, C_P2, C_T1, C_T2, C_TM2, C_T0 = range(8)
N_CHUNK = 8
TILE = 256


def dot(a, b, dims):
    return lax.dot_general(a, b, dims, preferred_element_type=jnp.float32)


def kernel(n_group, ell_ref, s_ref, x_ref, v_ref, y_ref, xs, vt, nrm, arep, acc, rx,
           load_sem, x_send, x_recv, v_send, v_recv, n_send, n_recv, t0_sem, r_send, r_recv):
    n_rows = x_ref.shape[0]
    n_chip = n_group // 2
    me = lax.axis_index('group')
    chip, core = me // 2, me % 2
    up = ((chip + 1) % n_chip) * 2 + core
    down = ((chip + n_chip - 1) % n_chip) * 2 + core
    partner = chip * 2 + 1 - core
    far = chip // (n_chip // 2)
    far_w = M2 + (P2 - M2) * far
    far_l = P2 - (P2 - M2) * far
    far_t = T2 + (TM2 - T2) * far

    def rows_of(j):
        return pl.ds(pl.multiple_of(j * TILE, TILE), TILE)

    def flip(j):
        return (j + N_CHUNK // 2) % N_CHUNK

    SRC = {C_M1: OWN, C_P1: OWN, C_M2: M1, C_P2: P1, C_T1: P1, C_T2: P2, C_TM2: M2, C_T0: OWN}
    DST = {C_M1: M1, C_P1: P1, C_M2: M2, C_P2: P2, C_T1: T1, C_T2: T2, C_TM2: TM2, C_T0: T0}
    TO = {C_M1: up, C_P1: down, C_M2: up, C_P2: down, C_T1: partner, C_T2: partner, C_TM2: partner, C_T0: partner}

    def x_copy(c, j):
        return pltpu.make_async_remote_copy(
            src_ref=xs.at[SRC[c], rows_of(j)], dst_ref=xs.at[DST[c], rows_of(j)],
            send_sem=x_send.at[c, j], recv_sem=x_recv.at[c, j],
            device_id={'group': TO[c]}, device_id_type=MESH)

    def t0_copy():
        return pltpu.make_async_remote_copy(
            src_ref=xs.at[OWN], dst_ref=xs.at[T0], send_sem=t0_sem.at[0], recv_sem=t0_sem.at[1],
            device_id={'group': partner}, device_id_type=MESH)

    def v_copy(c):
        src = v_ref if c in (C_M1, C_P1, C_T0) else vt.at[SRC[c]]
        return pltpu.make_async_remote_copy(
            src_ref=src, dst_ref=vt.at[DST[c]], send_sem=v_send.at[c], recv_sem=v_recv.at[c],
            device_id={'group': TO[c]}, device_id_type=MESH)

    def n_copy(c):
        return pltpu.make_async_remote_copy(
            src_ref=nrm.at[SRC[c]], dst_ref=nrm.at[DST[c]], send_sem=n_send.at[c], recv_sem=n_recv.at[c],
            device_id={'group': TO[c]}, device_id_type=MESH)

    def r_copy(src, i, to):
        return pltpu.make_async_remote_copy(
            src_ref=acc.at[src], dst_ref=rx.at[i], send_sem=r_send.at[i], recv_sem=r_recv.at[i],
            device_id={'group': to}, device_id_type=MESH)

    def load(j):
        return pltpu.make_async_copy(x_ref.at[rows_of(j)], xs.at[OWN, rows_of(j)], load_sem.at[j])

    for j in range(N_CHUNK):
        load(j).start()
    barrier = pltpu.get_barrier_semaphore()
    for peer in (up, down, partner):
        pl.semaphore_signal(barrier, inc=1, device_id={'group': peer}, device_id_type=MESH)
    pl.semaphore_wait(barrier, 3)
    for c in (C_M1, C_P1, C_T0):
        v_copy(c).start()
    for j in range(N_CHUNK):
        load(j).wait()
    for j in range(N_CHUNK):
        x_copy(C_M1, j).start()
        x_copy(C_P1, flip(j)).start()
    t0_copy().start()

    ell = jnp.full((1, 128), ell_ref[0], jnp.float32)
    coef = LOG2E / (2.0 * jnp.square(ell))
    top = LOG2E * jnp.log(jnp.full((1, 128), s_ref[0], jnp.float32))

    acc[...] = jnp.zeros_like(acc)
    vt[OWN] = v_ref[...]

    def own_norms(b, _):
        rows = pl.ds(pl.multiple_of(b * 128, 128), 128)
        part = jnp.sum(jnp.square(xs[OWN, rows, :].astype(jnp.float32)), axis=1, keepdims=True)
        part = jnp.broadcast_to(part, (128, 128))
        arep[R_OWN, rows, :] = part * coef - top
        nrm[OWN, :, rows] = part.T[0:1, :]
        return 0

    lax.fori_loop(0, n_rows // 128, own_norms, 0)

    def column_norms(slot, rep):
        def one(b, _):
            rows = pl.ds(pl.multiple_of(b * 128, 128), 128)
            row = jnp.broadcast_to(nrm[slot, :, rows], (128, 128))
            arep[rep, rows, :] = row.T * coef - top
            return 0
        lax.fori_loop(0, n_rows // 128, one, 0)

    def wide(v, n):
        return jnp.concatenate([v] * (n // 128), axis=1)

    def kern_of(left, shift, w, cols, n):
        gram = dot(left, xs[w, cols, :], NT)
        expo = gram * wide(2.0 * coef, n) - wide(shift, n) - nrm[w, :, cols] * wide(coef, n)
        return jnp.exp2(jnp.minimum(expo, wide(top, n))).astype(jnp.bfloat16)

    def pair(la, ja, ra, lb, jb, rb, w, base, n, sides=True, yw=None):
        cols = pl.ds(pl.multiple_of(base, TILE), n)
        a, b = rows_of(ja), rows_of(jb)
        left = jnp.concatenate([xs[la, a, :], xs[lb, b, :]], axis=0)
        shift = jnp.concatenate([arep[ra, a, :], arep[rb, b, :]], axis=0)
        kern = kern_of(left, shift, w, cols, n)
        v = jnp.concatenate([vt[la, :, a], vt[lb, :, b]], axis=1)
        acc[w, :, cols] += dot(v, kern, NN)
        if sides:
            y = dot(vt[w, :, cols], kern, NT)
            acc[la, :, a] += y[:, :TILE]
            acc[lb, :, b] += y[:, TILE:]

    def single(la, ja, ra, w):
        a = rows_of(ja)
        kern = kern_of(xs[la, a, :], arep[ra, a, :], w, slice(None), n_rows)
        acc[w] += dot(vt[la, :, a], kern, NN)
        acc[la, :, a] += dot(vt[w], kern, NT)

    def own_pairs(slot, rep):
        def one(i, _):
            pair(slot, 2 * i, rep, slot, 2 * i + 1, rep, OWN, 0, n_rows, sides=False)
            return 0
        lax.fori_loop(0, N_CHUNK // 2, one, 0)

    own_pairs(OWN, R_OWN)
    for c in (C_M1, C_P1, C_T0):
        n_copy(c).start()
    v_copy(C_T0).wait_recv()
    n_copy(C_T0).wait_recv()
    t0_copy().wait_recv()
    column_norms(T0, R_T0)
    v_copy(C_M1).wait_recv()
    n_copy(C_M1).wait_recv()
    v_copy(C_P1).wait_recv()
    n_copy(C_P1).wait_recv()
    for c in (C_M2, C_P2, C_T1):
        v_copy(c).start()
        n_copy(c).start()
    own_pairs(T0, R_T0)
    column_norms(P1, R_P1)
    v_copy(C_T1).wait_recv()
    n_copy(C_T1).wait_recv()
    column_norms(T1, R_T1)

    def mid(i, start):
        k = flip(i)
        pair(P1, k, R_P1, T1, k, R_T1, M1, start, n_rows // 2)

    def near_step(j, _):
        @pl.when(j < N_CHUNK)
        def _():
            k = flip(j)
            x_copy(C_P1, k).wait_recv()
            x_copy(C_T1, k).start()
            x_copy(C_P2, k).start()
            x_copy(C_M1, j).wait_recv()
            x_copy(C_M2, j).start()

        @pl.when(j > 0)
        def _():
            i = j - 1
            k = flip(i)
            x_copy(C_T1, k).wait_recv()
            pair(P1, k, R_P1, T1, k, R_T1, OWN, 0, n_rows)

            def one(i, _):
                mid(i, 0)
                return 0
            lax.fori_loop(jnp.where(j < 4, N_CHUNK, jnp.where(j == 4, 0, i)), jnp.where(j < 4, N_CHUNK, j), one, 0)
        return 0

    lax.fori_loop(0, N_CHUNK + 1, near_step, 0)

    for c in (C_M2, C_P2):
        v_copy(c).wait_recv()
        n_copy(c).wait_recv()
    for c in (C_T2, C_TM2):
        v_copy(c).start()
        n_copy(c).start()
    column_norms(P2, R_P2)
    mid(N_CHUNK - 1, n_rows // 2)
    for c in (C_T2, C_TM2):
        v_copy(c).wait_recv()
        n_copy(c).wait_recv()
    column_norms(T2, R_T2)
    column_norms(far_l, R_FAR)
    column_norms(far_t, R_TFAR)

    def arrive(j):
        k = flip(j)
        x_copy(C_P2, k).wait_recv()
        x_copy(C_T2, k).start()
        x_copy(C_M2, j).wait_recv()
        x_copy(C_TM2, j).start()

    def far_pair(i):
        q = jnp.where(far == 0, flip(i), i)
        pair(far_l, q, R_FAR, far_t, q, R_TFAR, far_w, far * (n_rows // 2), n_rows // 2)

    def far_step(j, _):
        k = flip(j)
        arrive(j)
        mid(j, n_rows // 2)
        x_copy(C_T2, k).wait_recv()
        x_copy(C_TM2, j).wait_recv()
        pair(P2, k, R_P2, T2, k, R_T2, M1, 0, n_rows)

        def one(i, _):
            far_pair(i)
            return 0
        lax.fori_loop(jnp.where(j < 3, N_CHUNK, jnp.where(j == 3, 0, j)), jnp.where(j < 3, N_CHUNK, j + 1), one, 0)
        return 0

    lax.fori_loop(0, N_CHUNK - 1, far_step, 0)

    ways = ((T1, partner), (T2, partner), (TM2, partner), (M2, down), (P2, up), (M1, down), (P1, up))

    def back(i):
        return r_copy(ways[i][0], i, ways[i][1])

    back(0).start()
    final = N_CHUNK - 1
    arrive(final)
    single(P2, flip(final), R_P2, M1)
    x_copy(C_T2, flip(final)).wait_recv()
    single(T2, flip(final), R_T2, M1)
    x_copy(C_TM2, final).wait_recv()
    far_pair(final)
    back(2).start()
    back(1).start()
    back(2).wait_recv()
    acc[M2] += rx[2]
    back(3).start()
    back(1).wait_recv()
    acc[P2] += rx[1]
    back(4).start()
    back(0).wait_recv()
    acc[P1] += rx[0]
    back(3).wait_recv()
    acc[M1] += rx[3]
    back(5).start()
    back(4).wait_recv()
    acc[P1] += rx[4]
    back(6).start()
    back(5).wait_recv()
    back(6).wait_recv()
    y_ref[...] = acc[OWN] + rx[5] + rx[6]

    def drain(j, _):
        for c in (C_M1, C_P1, C_M2, C_P2, C_T1, C_T2, C_TM2):
            x_copy(c, j).wait_send()
        return 0
    lax.fori_loop(0, N_CHUNK, drain, 0)
    t0_copy().wait_send()
    for c in range(8):
        v_copy(c).wait_send()
        n_copy(c).wait_send()
    for i in range(len(ways)):
        back(i).wait_send()


def solution(mesh):
    n_group = mesh.shape['group']
    row_spec = P(('tasks', 'group'), None)

    def local_fn(x_loc, v_loc, lengthscale, outscale):
        n_rows, n_feat = x_loc.shape
        n_rhs = v_loc.shape[1]
        smem = pl.BlockSpec(memory_space=pltpu.SMEM)
        vmem = pl.BlockSpec(memory_space=pltpu.VMEM)

        def body(*refs):
            kernel(n_group, *refs)

        y_t = pl.pallas_call(
            body,
            name='gauss_ring',
            out_shape=jax.ShapeDtypeStruct((n_rhs, n_rows), jnp.float32),
            in_specs=[smem, smem, pl.BlockSpec(memory_space=pl.ANY), vmem],
            out_specs=vmem,
            scratch_shapes=[
                pltpu.VMEM((N_SLOT, n_rows, n_feat), jnp.bfloat16),
                pltpu.VMEM((N_SLOT, n_rhs, n_rows), jnp.bfloat16),
                pltpu.VMEM((N_SLOT, 1, n_rows), jnp.float32),
                pltpu.VMEM((N_REP, n_rows, 128), jnp.float32),
                pltpu.VMEM((N_SLOT, n_rhs, n_rows), jnp.float32),
                pltpu.VMEM((7, n_rhs, n_rows), jnp.float32),
                pltpu.SemaphoreType.DMA((N_CHUNK,)),
                pltpu.SemaphoreType.DMA((7, N_CHUNK)),
                pltpu.SemaphoreType.DMA((7, N_CHUNK)),
                pltpu.SemaphoreType.DMA((8,)),
                pltpu.SemaphoreType.DMA((8,)),
                pltpu.SemaphoreType.DMA((8,)),
                pltpu.SemaphoreType.DMA((8,)),
                pltpu.SemaphoreType.DMA((2,)),
                pltpu.SemaphoreType.DMA((7,)),
                pltpu.SemaphoreType.DMA((7,)),
            ],
            compiler_params=pltpu.CompilerParams(
                collective_id=0, has_side_effects=True, vmem_limit_bytes=58 * 2**20),
        )(lengthscale, outscale, x_loc, v_loc.T)
        return y_t.T

    return jax.shard_map(local_fn, mesh=mesh, in_specs=(row_spec, row_spec, P(None), P(None)), out_specs=row_spec, check_vma=False)
```

time: 221 us -> 160 us (0.72)
  Pallas kernels: 218 us -> 157 us
    pallas_call x1, Pallas kernels: 218 us -> 157 us  [local_fn(): pl.pallas_call(body, name='gauss_ring', out_shape=jax.ShapeDtypeStruct((n...]
where the time goes in v2:
time: 160 us
  Pallas kernels  157 us (98%)
    pallas_call x1, Pallas kernels, local_fn(): pl.pallas_call(body, name='gauss_ring', out_shape=jax.ShapeDtypeStruct((n...  157 us

profile of v2, /device:TPU:22, one launch (start us, length us, event | category | flops | bytes accessed | tf_op | source)
XLA Modules:
  0.0 160.3 jit_solution(10415260331503852104)
XLA Ops:
  1.3 157.4 %gauss_ring.1 = f32[16,2048]{1,0:T(8,128)} custom-call(f32[1]{0:T(128)S(6)} %copy.6.refs_0_, f32[1]{0:T(128)S(6)} %copy.7.refs_1_, bf16[2048,512]{1,0:T(8,128)(2,1)} %refs_2_.1, bf16[16,2048]{1,0:T(8,128)(2,1)} %bitcast.3), custom_call_target="tpu_custom_call" | custom-call | tf_op jit(solution)/shard_map/gauss_ring/pallas_call | solution.py:302
  158.7 1.6 copy.8

commit v3 on v2

--- a/solution.py
+++ b/solution.py
@@ -86,9 +86,13 @@
         v_copy(c).start()
     for j in range(N_CHUNK):
         load(j).wait()
-    for j in range(N_CHUNK):
-        x_copy(C_M1, j).start()
-        x_copy(C_P1, flip(j)).start()
+
+    def send_own(first, last):
+        for j in range(first, last):
+            x_copy(C_M1, j).start()
+            x_copy(C_P1, flip(j)).start()
+
+    send_own(0, 1)
     t0_copy().start()
 
     ell = jnp.full((1, 128), ell_ref[0], jnp.float32)
@@ -98,23 +102,21 @@
     acc[...] = jnp.zeros_like(acc)
     vt[OWN] = v_ref[...]
 
-    def own_norms(b, _):
-        rows = pl.ds(pl.multiple_of(b * 128, 128), 128)
+    for b in range(n_rows // 128):
+        rows = slice(b * 128, (b + 1) * 128)
         part = jnp.sum(jnp.square(xs[OWN, rows, :].astype(jnp.float32)), axis=1, keepdims=True)
         part = jnp.broadcast_to(part, (128, 128))
         arep[R_OWN, rows, :] = part * coef - top
         nrm[OWN, :, rows] = part.T[0:1, :]
-        return 0
-
-    lax.fori_loop(0, n_rows // 128, own_norms, 0)
+    for c in (C_M1, C_P1, C_T0):
+        n_copy(c).start()
+    send_own(1, N_CHUNK // 2)
 
     def column_norms(slot, rep):
-        def one(b, _):
-            rows = pl.ds(pl.multiple_of(b * 128, 128), 128)
+        for b in range(n_rows // 128):
+            rows = slice(b * 128, (b + 1) * 128)
             row = jnp.broadcast_to(nrm[slot, :, rows], (128, 128))
             arep[rep, rows, :] = row.T * coef - top
-            return 0
-        lax.fori_loop(0, n_rows // 128, one, 0)
 
     def wide(v, n):
         return jnp.concatenate([v] * (n // 128), axis=1)
@@ -150,20 +152,18 @@
         lax.fori_loop(0, N_CHUNK // 2, one, 0)
 
     own_pairs(OWN, R_OWN)
-    for c in (C_M1, C_P1, C_T0):
-        n_copy(c).start()
     v_copy(C_T0).wait_recv()
     n_copy(C_T0).wait_recv()
     t0_copy().wait_recv()
     column_norms(T0, R_T0)
-    v_copy(C_M1).wait_recv()
-    n_copy(C_M1).wait_recv()
-    v_copy(C_P1).wait_recv()
-    n_copy(C_P1).wait_recv()
+    own_pairs(T0, R_T0)
+    for c in (C_M1, C_P1):
+        v_copy(c).wait_recv()
+        n_copy(c).wait_recv()
     for c in (C_M2, C_P2, C_T1):
         v_copy(c).start()
         n_copy(c).start()
-    own_pairs(T0, R_T0)
+    send_own(N_CHUNK // 2, N_CHUNK)
     column_norms(P1, R_P1)
     v_copy(C_T1).wait_recv()
     n_copy(C_T1).wait_recv()
@@ -196,8 +196,7 @@
             lax.fori_loop(jnp.where(j < 4, N_CHUNK, jnp.where(j == 4, 0, i)), jnp.where(j < 4, N_CHUNK, j), one, 0)
         return 0
 
-    lax.fori_loop(0, N_CHUNK + 1, near_step, 0)
-
+    lax.fori_loop(0, N_CHUNK - 2, near_step, 0)
     for c in (C_M2, C_P2):
         v_copy(c).wait_recv()
         n_copy(c).wait_recv()
@@ -205,13 +204,15 @@
         v_copy(c).start()
         n_copy(c).start()
     column_norms(P2, R_P2)
-    mid(N_CHUNK - 1, n_rows // 2)
     for c in (C_T2, C_TM2):
         v_copy(c).wait_recv()
         n_copy(c).wait_recv()
     column_norms(T2, R_T2)
     column_norms(far_l, R_FAR)
     column_norms(far_t, R_TFAR)
+    lax.fori_loop(N_CHUNK - 2, N_CHUNK + 1, near_step, 0)
+
+    mid(N_CHUNK - 1, n_rows // 2)
 
     def arrive(j):
         k = flip(j)

time: 160 us -> 126 us (0.79)
  Pallas kernels: 157 us -> 123 us
    pallas_call x1, Pallas kernels: 157 us -> 123 us  [local_fn(): pl.pallas_call(body, name='gauss_ring', out_shape=jax.ShapeDtypeStruct((n...]
where the time goes in v3:
time: 126 us
  Pallas kernels  123 us (98%)
  local copies, waits for them, and re-layouts  1.57 us (1%)
  between operations  1.31 us (1%)
    pallas_call x1, Pallas kernels, local_fn(): pl.pallas_call(body, name='gauss_ring', out_shape=jax.ShapeDtypeStruct((n...  123 us

profile of v3, /device:TPU:22, one launch (start us, length us, event | category | flops | bytes accessed | tf_op | source)
XLA Modules:
  0.0 126.0 jit_solution(10387676072259555516)
XLA Ops:
  1.3 123.1 %gauss_ring.1 = f32[16,2048]{1,0:T(8,128)} custom-call(f32[1]{0:T(128)S(6)} %copy.6.refs_0_, f32[1]{0:T(128)S(6)} %copy.7.refs_1_, bf16[2048,512]{1,0:T(8,128)(2,1)} %refs_2_.1, bf16[16,2048]{1,0:T(8,128)(2,1)} %bitcast.3), custom_call_target="tpu_custom_call" | custom-call | tf_op jit(solution)/shard_map/gauss_ring/pallas_call | solution.py:303
  124.4 1.6 %copy.8 = f32[2048,16]{0,1:T(8,128)} copy(f32[2048,16]{0,1:T(8,128)} %bitcast.2) | data formatting | bytes 262144

commit v4 on v3

--- a/solution.py
+++ b/solution.py
@@ -16,6 +16,7 @@
 C_M1, C_P1, C_M2, C_P2, C_T1, C_T2, C_TM2, C_T0 = range(8)
 N_CHUNK = 8
 TILE = 256
+N_PIECE = 4
 
 
 def dot(a, b, dims):
@@ -68,15 +69,20 @@
             src_ref=nrm.at[SRC[c]], dst_ref=nrm.at[DST[c]], send_sem=n_send.at[c], recv_sem=n_recv.at[c],
             device_id={'group': TO[c]}, device_id_type=MESH)
 
-    def r_copy(src, i, to):
-        return pltpu.make_async_remote_copy(
-            src_ref=acc.at[src], dst_ref=rx.at[i], send_sem=r_send.at[i], recv_sem=r_recv.at[i],
+    def piece(p):
+        return slice(p * n_rows // N_PIECE, (p + 1) * n_rows // N_PIECE)
+
+    def r_copy(src, i, to, p):
+        return pltpu.make_async_remote_copy(
+            src_ref=acc.at[src, :, piece(p)], dst_ref=rx.at[i, :, piece(p)],
+            send_sem=r_send.at[i, p], recv_sem=r_recv.at[i, p],
             device_id={'group': to}, device_id_type=MESH)
 
     def load(j):
         return pltpu.make_async_copy(x_ref.at[rows_of(j)], xs.at[OWN, rows_of(j)], load_sem.at[j])
 
-    for j in range(N_CHUNK):
+    order = [j for i in range(N_CHUNK // 2) for j in (i, flip(i))]
+    for j in order:
         load(j).start()
     barrier = pltpu.get_barrier_semaphore()
     for peer in (up, down, partner):
@@ -84,15 +90,16 @@
     pl.semaphore_wait(barrier, 3)
     for c in (C_M1, C_P1, C_T0):
         v_copy(c).start()
-    for j in range(N_CHUNK):
-        load(j).wait()
-
     def send_own(first, last):
         for j in range(first, last):
             x_copy(C_M1, j).start()
             x_copy(C_P1, flip(j)).start()
 
+    for j in order[:2]:
+        load(j).wait()
     send_own(0, 1)
+    for j in order[2:]:
+        load(j).wait()
     t0_copy().start()
 
     ell = jnp.full((1, 128), ell_ref[0], jnp.float32)
@@ -138,12 +145,6 @@
             y = dot(vt[w, :, cols], kern, NT)
             acc[la, :, a] += y[:, :TILE]
             acc[lb, :, b] += y[:, TILE:]
-
-    def single(la, ja, ra, w):
-        a = rows_of(ja)
-        kern = kern_of(xs[la, a, :], arep[ra, a, :], w, slice(None), n_rows)
-        acc[w] += dot(vt[la, :, a], kern, NN)
-        acc[la, :, a] += dot(vt[w], kern, NT)
 
     def own_pairs(slot, rep):
         def one(i, _):
@@ -221,6 +222,10 @@
         x_copy(C_M2, j).wait_recv()
         x_copy(C_TM2, j).start()
 
+    def last_near(j):
+        k = flip(N_CHUNK - 1)
+        pair(P1, k, R_P1, T1, k, R_T1, M2, j * TILE, TILE)
+
     def far_pair(i):
         q = jnp.where(far == 0, flip(i), i)
         pair(far_l, q, R_FAR, far_t, q, R_TFAR, far_w, far * (n_rows // 2), n_rows // 2)
@@ -229,6 +234,7 @@
         k = flip(j)
         arrive(j)
         mid(j, n_rows // 2)
+        last_near(j)
         x_copy(C_T2, k).wait_recv()
         x_copy(C_TM2, j).wait_recv()
         pair(P2, k, R_P2, T2, k, R_T2, M1, 0, n_rows)
@@ -241,38 +247,45 @@
 
     lax.fori_loop(0, N_CHUNK - 1, far_step, 0)
 
-    ways = ((T1, partner), (T2, partner), (TM2, partner), (M2, down), (P2, up), (M1, down), (P1, up))
-
-    def back(i):
-        return r_copy(ways[i][0], i, ways[i][1])
-
-    back(0).start()
     final = N_CHUNK - 1
     arrive(final)
-    single(P2, flip(final), R_P2, M1)
+    last_near(final)
     x_copy(C_T2, flip(final)).wait_recv()
-    single(T2, flip(final), R_T2, M1)
     x_copy(C_TM2, final).wait_recv()
     far_pair(final)
-    back(2).start()
-    back(1).start()
-    back(2).wait_recv()
-    acc[M2] += rx[2]
-    back(3).start()
-    back(1).wait_recv()
-    acc[P2] += rx[1]
-    back(4).start()
-    back(0).wait_recv()
-    acc[P1] += rx[0]
-    back(3).wait_recv()
-    acc[M1] += rx[3]
-    back(5).start()
-    back(4).wait_recv()
-    acc[P1] += rx[4]
-    back(6).start()
-    back(5).wait_recv()
-    back(6).wait_recv()
-    y_ref[...] = acc[OWN] + rx[5] + rx[6]
+
+    ways = ((T1, partner), (T2, partner), (TM2, partner), (M2, down), (P2, up), (M1, down), (P1, up))
+    pieces = range(N_PIECE)
+
+    def back(i, p):
+        return r_copy(ways[i][0], i, ways[i][1], p)
+
+    for p in pieces:
+        back(2, p).start()
+        back(1, p).start()
+    for p in pieces:
+        back(0, p).start()
+    for p in pieces:
+        back(2, p).wait_recv()
+        acc[M2, :, piece(p)] += rx[2, :, piece(p)]
+        back(3, p).start()
+        back(1, p).wait_recv()
+        acc[P2, :, piece(p)] += rx[1, :, piece(p)]
+        back(4, p).start()
+    for p in pieces:
+        back(0, p).wait_recv()
+        acc[P1, :, piece(p)] += rx[0, :, piece(p)]
+    for p in pieces:
+        back(3, p).wait_recv()
+        acc[M1, :, piece(p)] += rx[3, :, piece(p)]
+        back(5, p).start()
+        back(4, p).wait_recv()
+        acc[P1, :, piece(p)] += rx[4, :, piece(p)]
+        back(6, p).start()
+    for p in pieces:
+        back(5, p).wait_recv()
+        back(6, p).wait_recv()
+        y_ref[:, piece(p)] = acc[OWN, :, piece(p)] + rx[5, :, piece(p)] + rx[6, :, piece(p)]
 
     def drain(j, _):
         for c in (C_M1, C_P1, C_M2, C_P2, C_T1, C_T2, C_TM2):
@@ -284,7 +297,8 @@
         v_copy(c).wait_send()
         n_copy(c).wait_send()
     for i in range(len(ways)):
-        back(i).wait_send()
+        for p in pieces:
+            back(i, p).wait_send()
 
 
 def solution(mesh):
@@ -321,8 +335,8 @@
                 pltpu.SemaphoreType.DMA((8,)),
                 pltpu.SemaphoreType.DMA((8,)),
                 pltpu.SemaphoreType.DMA((2,)),
-                pltpu.SemaphoreType.DMA((7,)),
-                pltpu.SemaphoreType.DMA((7,)),
+                pltpu.SemaphoreType.DMA((7, N_PIECE)),
+                pltpu.SemaphoreType.DMA((7, N_PIECE)),
             ],
             compiler_params=pltpu.CompilerParams(
                 collective_id=0, has_side_effects=True, vmem_limit_bytes=58 * 2**20),

time: 126 us -> 125 us (level)
    pallas_call x1, Pallas kernels: 123 us -> 122 us  [local_fn(): pl.pallas_call(body, name='gauss_ring', out_shape=jax.ShapeDtypeStruct((n...]
where the time goes in v4:
time: 125 us
  Pallas kernels  122 us (98%)
  local copies, waits for them, and re-layouts  1.57 us (1%)
  between operations  1.31 us (1%)
    pallas_call x1, Pallas kernels, local_fn(): pl.pallas_call(body, name='gauss_ring', out_shape=jax.ShapeDtypeStruct((n...  122 us

profile of v4, /device:TPU:22, one launch (start us, length us, event | category | flops | bytes accessed | tf_op | source)
XLA Modules:
  0.0 124.6 jit_solution(4389538290660473911)
XLA Ops:
  1.3 121.7 %gauss_ring.1 = f32[16,2048]{1,0:T(8,128)} custom-call(f32[1]{0:T(128)S(6)} %copy.6.refs_0_, f32[1]{0:T(128)S(6)} %copy.7.refs_1_, bf16[2048,512]{1,0:T(8,128)(2,1)} %refs_2_.1, bf16[16,2048]{1,0:T(8,128)(2,1)} %bitcast.3), custom_call_target="tpu_custom_call" | custom-call | tf_op jit(solution)/shard_map/gauss_ring/pallas_call | solution.py:317
  123.0 1.6 %copy.8 = f32[2048,16]{0,1:T(8,128)} copy(f32[2048,16]{0,1:T(8,128)} %bitcast.2) | data formatting | bytes 262144

commit v5 on v4

--- a/solution.py
+++ b/solution.py
@@ -23,8 +23,8 @@
     return lax.dot_general(a, b, dims, preferred_element_type=jnp.float32)
 
 
-def kernel(n_group, ell_ref, s_ref, x_ref, v_ref, y_ref, xs, vt, nrm, arep, acc, rx,
-           load_sem, x_send, x_recv, v_send, v_recv, n_send, n_recv, t0_sem, r_send, r_recv):
+def kernel(n_group, ell_ref, s_ref, x_ref, v_ref, y_ref, y_vmem, xs, vt, nrm, arep, acc, rx,
+           v_sem, y_sem, load_sem, x_send, x_recv, v_send, v_recv, n_send, n_recv, t0_sem, r_send, r_recv):
     n_rows = x_ref.shape[0]
     n_chip = n_group // 2
     me = lax.axis_index('group')
@@ -59,9 +59,8 @@
             device_id={'group': partner}, device_id_type=MESH)
 
     def v_copy(c):
-        src = v_ref if c in (C_M1, C_P1, C_T0) else vt.at[SRC[c]]
-        return pltpu.make_async_remote_copy(
-            src_ref=src, dst_ref=vt.at[DST[c]], send_sem=v_send.at[c], recv_sem=v_recv.at[c],
+        return pltpu.make_async_remote_copy(
+            src_ref=vt.at[SRC[c]], dst_ref=vt.at[DST[c]], send_sem=v_send.at[c], recv_sem=v_recv.at[c],
             device_id={'group': TO[c]}, device_id_type=MESH)
 
     def n_copy(c):
@@ -81,6 +80,8 @@
     def load(j):
         return pltpu.make_async_copy(x_ref.at[rows_of(j)], xs.at[OWN, rows_of(j)], load_sem.at[j])
 
+    load_v = pltpu.make_async_copy(v_ref, vt.at[OWN], v_sem)
+    load_v.start()
     order = [j for i in range(N_CHUNK // 2) for j in (i, flip(i))]
     for j in order:
         load(j).start()
@@ -88,6 +89,7 @@
     for peer in (up, down, partner):
         pl.semaphore_signal(barrier, inc=1, device_id={'group': peer}, device_id_type=MESH)
     pl.semaphore_wait(barrier, 3)
+    load_v.wait()
     for c in (C_M1, C_P1, C_T0):
         v_copy(c).start()
     def send_own(first, last):
@@ -107,7 +109,6 @@
     top = LOG2E * jnp.log(jnp.full((1, 128), s_ref[0], jnp.float32))
 
     acc[...] = jnp.zeros_like(acc)
-    vt[OWN] = v_ref[...]
 
     for b in range(n_rows // 128):
         rows = slice(b * 128, (b + 1) * 128)
@@ -257,6 +258,9 @@
     ways = ((T1, partner), (T2, partner), (TM2, partner), (M2, down), (P2, up), (M1, down), (P1, up))
     pieces = range(N_PIECE)
 
+    def y_out(p):
+        return pltpu.make_async_copy(y_vmem.at[:, piece(p)], y_ref.at[:, piece(p)], y_sem.at[p])
+
     def back(i, p):
         return r_copy(ways[i][0], i, ways[i][1], p)
 
@@ -285,7 +289,8 @@
     for p in pieces:
         back(5, p).wait_recv()
         back(6, p).wait_recv()
-        y_ref[:, piece(p)] = acc[OWN, :, piece(p)] + rx[5, :, piece(p)] + rx[6, :, piece(p)]
+        y_vmem[:, piece(p)] = acc[OWN, :, piece(p)] + rx[5, :, piece(p)] + rx[6, :, piece(p)]
+        y_out(p).start()
 
     def drain(j, _):
         for c in (C_M1, C_P1, C_M2, C_P2, C_T1, C_T2, C_TM2):
@@ -299,6 +304,8 @@
     for i in range(len(ways)):
         for p in pieces:
             back(i, p).wait_send()
+    for p in pieces:
+        y_out(p).wait()
 
 
 def solution(mesh):
@@ -309,7 +316,7 @@
         n_rows, n_feat = x_loc.shape
         n_rhs = v_loc.shape[1]
         smem = pl.BlockSpec(memory_space=pltpu.SMEM)
-        vmem = pl.BlockSpec(memory_space=pltpu.VMEM)
+        hbm = pl.BlockSpec(memory_space=pl.ANY)
 
         def body(*refs):
             kernel(n_group, *refs)
@@ -318,15 +325,18 @@
             body,
             name='gauss_ring',
             out_shape=jax.ShapeDtypeStruct((n_rhs, n_rows), jnp.float32),
-            in_specs=[smem, smem, pl.BlockSpec(memory_space=pl.ANY), vmem],
-            out_specs=vmem,
+            in_specs=[smem, smem, hbm, hbm],
+            out_specs=hbm,
             scratch_shapes=[
+                pltpu.VMEM((n_rhs, n_rows), jnp.float32),
                 pltpu.VMEM((N_SLOT, n_rows, n_feat), jnp.bfloat16),
                 pltpu.VMEM((N_SLOT, n_rhs, n_rows), jnp.bfloat16),
                 pltpu.VMEM((N_SLOT, 1, n_rows), jnp.float32),
                 pltpu.VMEM((N_REP, n_rows, 128), jnp.float32),
                 pltpu.VMEM((N_SLOT, n_rhs, n_rows), jnp.float32),
                 pltpu.VMEM((7, n_rhs, n_rows), jnp.float32),
+                pltpu.SemaphoreType.DMA,
+                pltpu.SemaphoreType.DMA((N_PIECE,)),
                 pltpu.SemaphoreType.DMA((N_CHUNK,)),
                 pltpu.SemaphoreType.DMA((7, N_CHUNK)),
                 pltpu.SemaphoreType.DMA((7, N_CHUNK)),

time: 125 us -> 124 us (level)
  no operation moved by 1% of the time
where the time goes in v5:
time: 124 us
  Pallas kernels  121 us (98%)
  local copies, waits for them, and re-layouts  1.57 us (1%)
  between operations  1.31 us (1%)
    pallas_call x1, Pallas kernels, local_fn(): pl.pallas_call(body, name='gauss_ring', out_shape=jax.ShapeDtypeStruct((n...  121 us

profile of v5, /device:TPU:22, one launch (start us, length us, event | category | flops | bytes accessed | tf_op | source)
XLA Modules:
  0.0 124.3 jit_solution(18050121164980722981)
XLA Ops:
  1.3 121.4 %gauss_ring.1 = f32[16,2048]{1,0:T(8,128)} custom-call(f32[1]{0:T(128)S(6)} %copy.6.refs_0_, f32[1]{0:T(128)S(6)} %copy.7.refs_1_, bf16[2048,512]{1,0:T(8,128)(2,1)} %refs_2_.1, bf16[16,2048]{1,0:T(8,128)(2,1)} %bitcast.3), custom_call_target="tpu_custom_call" | custom-call | tf_op jit(solution)/shard_map/gauss_ring/pallas_call | solution.py:324
  122.7 1.6 %copy.8 = f32[2048,16]{0,1:T(8,128)} copy(f32[2048,16]{0,1:T(8,128)} %bitcast.2) | data formatting | bytes 262144

commit v6 on v5

--- a/solution.py
+++ b/solution.py
@@ -248,48 +248,56 @@
 
     lax.fori_loop(0, N_CHUNK - 1, far_step, 0)
 
+    ways = ((T1, partner), (T2, partner), (TM2, partner), (M2, down), (P2, up), (M1, down), (P1, up))
+    B_T1, B_T2, B_TM2, B_M2, B_P2, B_M1, B_P1 = range(7)
+    pieces = range(N_PIECE)
+
+    def y_out(p):
+        return pltpu.make_async_copy(y_vmem.at[:, piece(p)], y_ref.at[:, piece(p)], y_sem.at[p])
+
+    def back(i, p):
+        return r_copy(ways[i][0], i, ways[i][1], p)
+
+    def take(i, p, slot):
+        back(i, p).wait_recv()
+        acc[slot, :, piece(p)] += rx[i, :, piece(p)]
+
+    early = {B_TM2: (2, 0, 1), B_T2: (0, 2, 3), B_T1: (0, 2, 3)}
+    late = {B_TM2: 3, B_T2: 1, B_T1: 1}
+    home = {B_TM2: M2, B_T2: P2, B_T1: P1}
+    for i in early:
+        for p in early[i]:
+            back(i, p).start()
     final = N_CHUNK - 1
     arrive(final)
+    for i in early:
+        for p in early[i]:
+            take(i, p, home[i])
+    back(B_M2, 2).start()
+    back(B_P2, 0).start()
     last_near(final)
     x_copy(C_T2, flip(final)).wait_recv()
     x_copy(C_TM2, final).wait_recv()
     far_pair(final)
-
-    ways = ((T1, partner), (T2, partner), (TM2, partner), (M2, down), (P2, up), (M1, down), (P1, up))
-    pieces = range(N_PIECE)
-
-    def y_out(p):
-        return pltpu.make_async_copy(y_vmem.at[:, piece(p)], y_ref.at[:, piece(p)], y_sem.at[p])
-
-    def back(i, p):
-        return r_copy(ways[i][0], i, ways[i][1], p)
-
-    for p in pieces:
-        back(2, p).start()
-        back(1, p).start()
-    for p in pieces:
-        back(0, p).start()
-    for p in pieces:
-        back(2, p).wait_recv()
-        acc[M2, :, piece(p)] += rx[2, :, piece(p)]
-        back(3, p).start()
-        back(1, p).wait_recv()
-        acc[P2, :, piece(p)] += rx[1, :, piece(p)]
-        back(4, p).start()
-    for p in pieces:
-        back(0, p).wait_recv()
-        acc[P1, :, piece(p)] += rx[0, :, piece(p)]
-    for p in pieces:
-        back(3, p).wait_recv()
-        acc[M1, :, piece(p)] += rx[3, :, piece(p)]
-        back(5, p).start()
-        back(4, p).wait_recv()
-        acc[P1, :, piece(p)] += rx[4, :, piece(p)]
-        back(6, p).start()
-    for p in pieces:
-        back(5, p).wait_recv()
-        back(6, p).wait_recv()
-        y_vmem[:, piece(p)] = acc[OWN, :, piece(p)] + rx[5, :, piece(p)] + rx[6, :, piece(p)]
+    for i in late:
+        back(i, late[i]).start()
+    for p, q in ((0, 2), (1, 3)):
+        back(B_M2, p).start()
+        back(B_P2, q).start()
+    take(B_TM2, 3, M2)
+    back(B_M2, 3).start()
+    take(B_T2, 1, P2)
+    back(B_P2, 1).start()
+    take(B_T1, 1, P1)
+    for p, q in ((2, 0), (0, 2), (1, 3), (3, 1)):
+        take(B_M2, p, M1)
+        back(B_M1, p).start()
+        take(B_P2, q, P1)
+        back(B_P1, q).start()
+    for p in (0, 2, 1, 3):
+        back(B_M1, p).wait_recv()
+        back(B_P1, p).wait_recv()
+        y_vmem[:, piece(p)] = acc[OWN, :, piece(p)] + rx[B_M1, :, piece(p)] + rx[B_P1, :, piece(p)]
         y_out(p).start()
 
     def drain(j, _):

time: 124 us -> 123 us (level)
    pallas_call x1, Pallas kernels: 121 us -> 120 us  [local_fn(): pl.pallas_call(body, name='gauss_ring', out_shape=jax.ShapeDtypeStruct((n...]
where the time goes in v6:
time: 123 us
  Pallas kernels  120 us (98%)
  local copies, waits for them, and re-layouts  1.57 us (1%)
  between operations  1.31 us (1%)
    pallas_call x1, Pallas kernels, local_fn(): pl.pallas_call(body, name='gauss_ring', out_shape=jax.ShapeDtypeStruct((n...  120 us

profile of v6, /device:TPU:22, one launch (start us, length us, event | category | flops | bytes accessed | tf_op | source)
XLA Modules:
  0.0 123.0 jit_solution(11727574816091307271)
XLA Ops:
  1.3 120.1 %gauss_ring.1 = f32[16,2048]{1,0:T(8,128)} custom-call(f32[1]{0:T(128)S(6)} %copy.6.refs_0_, f32[1]{0:T(128)S(6)} %copy.7.refs_1_, bf16[2048,512]{1,0:T(8,128)(2,1)} %refs_2_.1, bf16[16,2048]{1,0:T(8,128)(2,1)} %bitcast.3), custom_call_target="tpu_custom_call" | custom-call | tf_op jit(solution)/shard_map/gauss_ring/pallas_call | solution.py:332
  121.4 1.6 %copy.8 = f32[2048,16]{0,1:T(8,128)} copy(f32[2048,16]{0,1:T(8,128)} %bitcast.2) | data formatting | bytes 262144

commit v7 on v6

--- a/solution.py
+++ b/solution.py
@@ -231,6 +231,14 @@
         q = jnp.where(far == 0, flip(i), i)
         pair(far_l, q, R_FAR, far_t, q, R_TFAR, far_w, far * (n_rows // 2), n_rows // 2)
 
+    def far_single(slot, j, rep):
+        n = n_rows // 2
+        cols = pl.ds(pl.multiple_of(far * n, TILE), n)
+        a = rows_of(j)
+        kern = kern_of(xs[slot, a, :], arep[rep, a, :], far_w, cols, n)
+        acc[far_w, :, cols] += dot(vt[slot, :, a], kern, NN)
+        acc[slot, :, a] += dot(vt[far_w, :, cols], kern, NT)
+
     def far_step(j, _):
         k = flip(j)
         arrive(j)
@@ -276,9 +284,11 @@
     back(B_M2, 2).start()
     back(B_P2, 0).start()
     last_near(final)
+    last = jnp.where(far == 0, flip(final), final)
+    far_single(far_l, last, R_FAR)
     x_copy(C_T2, flip(final)).wait_recv()
     x_copy(C_TM2, final).wait_recv()
-    far_pair(final)
+    far_single(far_t, last, R_TFAR)
     for i in late:
         back(i, late[i]).start()
     for p, q in ((0, 2), (1, 3)):

time: 123 us -> 123 us (level)
  no operation moved by 1% of the time
where the time goes in v7:
time: 123 us
  Pallas kernels  120 us (98%)
  local copies, waits for them, and re-layouts  1.57 us (1%)
  between operations  1.31 us (1%)
    pallas_call x1, Pallas kernels, local_fn(): pl.pallas_call(body, name='gauss_ring', out_shape=jax.ShapeDtypeStruct((n...  120 us

profile of v7, /device:TPU:22, one launch (start us, length us, event | category | flops | bytes accessed | tf_op | source)
XLA Modules:
  0.0 123.2 jit_solution(10377614617802416578)
XLA Ops:
  1.3 120.3 %gauss_ring.1 = f32[16,2048]{1,0:T(8,128)} custom-call(f32[1]{0:T(128)S(6)} %copy.6.refs_0_, f32[1]{0:T(128)S(6)} %copy.7.refs_1_, bf16[2048,512]{1,0:T(8,128)(2,1)} %refs_2_.1, bf16[16,2048]{1,0:T(8,128)(2,1)} %bitcast.3), custom_call_target="tpu_custom_call" | custom-call | tf_op jit(solution)/shard_map/gauss_ring/pallas_call | solution.py:342
  121.6 1.6 %copy.8 = f32[2048,16]{0,1:T(8,128)} copy(f32[2048,16]{0,1:T(8,128)} %bitcast.2) | data formatting | bytes 262144
